TPU v7x, 32 devices: a whole 2x2x4 slice. The times are simulated.
32 devices in a mesh: row: 8 (over y, x, core), col: 4 (over z).
Axes of the slice: x: 2, y: 2, z: 4, core: 2. Of those that a mesh axis runs over, the one named last changes fastest.
Arguments:
- query: bfloat16 [8, 512, 4096], P(None, 'col'), may hold values from -7 to 7
- key: bfloat16 [4096, 512], P(('row', 'col')), may hold values from -7 to 7
- value: bfloat16 [4096, 512], P(('row', 'col')), may hold values from -4 to 4
- span_order: int32 [32], replicated, may hold values from 0 to 31, each once
Outputs:
- attention: bfloat16 [4096, 4096], P(('row', 'col'))
Inputs may be any that keep to these rules, and one draw needn't show every extreme that they name: span_order is a permutation of 0 to 31.
All inputs are finite; a program needn't handle non-finite values.
Results may differ from a plain program's by a relative error of at most 0.0085.
Values may be sent and summed in bfloat16 or wider, within the bound.
A program may use at most 192 MiB of HBM per device.

v0:
```python
import jax
import jax.numpy as jnp
from jax import lax
from jax.sharding import PartitionSpec as P

HEAD_DIM = 128
QHEADS = 32
KVHEADS = 4


masked_score = -1e30


def passed_along(value, axis, steps):
    count = lax.axis_size(axis)
    pairs = [(source, (source + steps) % count) for source in range(count)]
    return lax.ppermute(value, axis, pairs)


def lookup(table, indices):
    columns = jnp.arange(table.shape[0], dtype=jnp.int32)
    chosen = jnp.where(indices[:, None] == columns[None, :], table[None, :], 0)
    return jnp.sum(chosen, axis=1)


def attend(state, queries, query_places, keys, values, key_places):
    best, total, summed = state
    scores = jnp.einsum(
        "nkgd,skd->nkgs", queries, keys, preferred_element_type=jnp.float32
    ) * queries.shape[-1] ** (-0.5)
    visible = key_places[None, None, None, :] <= query_places[:, None, None, None]
    scores = jnp.where(visible, scores, masked_score)
    newest = jnp.maximum(best, jnp.max(scores, axis=-1))
    shrink = jnp.exp(best - newest)
    raised = jnp.exp(scores - newest[..., None])
    total = jnp.sum(raised, axis=-1)
    weights = raised.astype(jnp.bfloat16)
    update = jnp.einsum("nkgs,skd->nkgd", weights, values, preferred_element_type=jnp.float32)
    summed = update
    return (newest, total, summed)


def finish(state):
    best, total, summed = state
    floor = jnp.maximum(total, 1.0)
    return ((summed / floor[..., None]).astype(jnp.bfloat16), best + jnp.log(floor))


def combine(partials, log_sums):
    highest = jnp.max(log_sums, axis=0)
    combined = highest + jnp.log(jnp.sum(jnp.exp(log_sums - highest), axis=0))
    scale_each = jnp.exp(log_sums - combined)
    return jnp.sum(scale_each[..., None] * partials.astype(jnp.float32), axis=0)


def empty_state(lead):
    best = jnp.full(lead, masked_score, jnp.float32)
    total = jnp.zeros(lead, jnp.float32)
    summed = jnp.zeros(lead + (HEAD_DIM,), jnp.float32)
    return (best, total, summed)


def shards(query, key, value, span_order):
    rows = lax.axis_size("row")
    columns = lax.axis_size("col")
    row_id = lax.axis_index("row")
    col_id = lax.axis_index("col")
    block_rows = key.shape[0]
    group = QHEADS // KVHEADS
    offsets = jnp.arange(block_rows, dtype=jnp.int32)
    tile_spans = jnp.arange(rows, dtype=jnp.int32) * columns + col_id
    tile_orders = lookup(span_order, tile_spans)
    tile_places = tile_orders[:, None] * block_rows + offsets[None, :]
    block_orders = lookup(span_order, row_id * columns + jnp.arange(columns, dtype=jnp.int32))
    block_places = block_orders[:, None] * block_rows + offsets[None, :]
    outputs = []
    for head in range(KVHEADS):
        low = head * group * HEAD_DIM
        high = (head + 1) * group * HEAD_DIM
        head_queries = query[:, :, low:high].reshape(rows, block_rows, 1, group, HEAD_DIM)
        head_keys = key[:, head * HEAD_DIM : (head + 1) * HEAD_DIM]
        head_values = value[:, head * HEAD_DIM : (head + 1) * HEAD_DIM]
        pair = jnp.stack([head_keys, head_values]).reshape(2, block_rows, 1, HEAD_DIM)
        held = jnp.zeros((columns,) + pair.shape, pair.dtype)

        def turn(step, carry):
            stored, moving = carry
            source = (col_id - step) % columns
            stored = lax.dynamic_update_index_in_dim(stored, moving, source, 0)
            moving = passed_along(moving, "col", 1)
            return (stored, moving)

        held, pair = lax.fori_loop(0, columns - 1, turn, (held, pair))
        held = lax.dynamic_update_index_in_dim(held, pair, (col_id - (columns - 1)) % columns, 0)

        def tile_step(unused, inputs, held=held):
            tile_queries, tile_spots, tile_order = inputs
            start_state = empty_state((block_rows, 1, group))
            all_keys = held[:, 0].reshape(columns * block_rows, 1, HEAD_DIM)
            all_values = held[:, 1].reshape(columns * block_rows, 1, HEAD_DIM)
            state = attend(
                start_state,
                tile_queries,
                tile_spots,
                all_keys,
                all_values,
                block_places.reshape(columns * block_rows),
            )
            return (unused, finish(state))

        unused, results = lax.scan(
            tile_step, jnp.int32(0), (head_queries, tile_places, tile_orders)
        )
        partial_value, log_sum = results
        partial_value = lax.all_to_all(
            partial_value.reshape(rows, block_rows, group * HEAD_DIM),
            "row",
            split_axis=0,
            concat_axis=0,
            tiled=True,
        )
        log_sum = lax.all_to_all(
            log_sum.reshape(rows, block_rows, group), "row", split_axis=0, concat_axis=0, tiled=True
        )
        merged = combine(
            partial_value.reshape(rows, block_rows, 1, group, HEAD_DIM),
            log_sum.reshape(rows, block_rows, 1, group),
        )
        outputs.append(merged.reshape(block_rows, group * HEAD_DIM))
    return jnp.concatenate(outputs, axis=1).astype(jnp.bfloat16)


def solution(mesh):
    placed = (P(None, "col", None), P(("row", "col"), None), P(("row", "col"), None), P())
    return jax.shard_map(
        shards, mesh=mesh, in_specs=placed, out_specs=P(("row", "col"), None), check_vma=False
    )
```

profile of v0, /device:TPU:1, one launch (start us, length us, event | category | flops | bytes accessed | tf_op | source)
XLA Modules:
  0.0 365.9 jit_solution(8904010601652355132)
XLA Ops:
  3.4 5.9 %fusion.68 = (bf16[8,128,1024]{2,1,0:T(8,128)(2,1)S(1)}, bf16[8,128,1024]{2,1,0:T(8,128)(2,1)}, bf16[8,128,1024]{2,1,0:T(8,128)(2,1)}, bf16[8,128,1024]{2,1,0:T(8,128)(2,1)}) fusion(bf16[8,128,4096]{2,1,0:T(8,128)(2,1)} %param.20), kind=kLoop, calls=%fused_computation.146 | loop fusion | bytes 16777216 | tf_op jit(solution)/shard_map/slice | solution.py:80
  9.3 2.4 copy.83
  11.8 15.7 %while.120 = (s32[]{:T(128)}, bf16[4,2,128,1,128]{4,2,0,3,1:T(8,128)(2,1)S(1)}, bf16[2,128,1,128]{3,1,0,2:T(8,128)(2,1)S(1)}, s32[]{:T(128)}, s32[]{:T(128)}, /*index=5*/s32[]{:T(128)}, s32[]{:T(128)}, s32[]{:T(128)}) while((s32[]{:T(128)}, bf16[4,2,128,1,128]{4,2,0,3,1:T(8,128)(2,1)S(1)}, bf16[2,128,1,128]{3,1,0,2:T(8,128)(2,1)S(1)}, ...), condition=%wide.region_2.3_spmd, body=%wide.region_1.2_spmd.sunk | while | flops 17 | bytes 524572 | solution.py:93
  11.8 2.2 collective-permute-start
  14.0 3.7 %collective-permute-done = bf16[2,128,1,128]{3,1,0,2:T(8,128)(2,1)S(1)} collective-permute-done((bf16[2,128,1,128]{3,1,0,2:T(8,128)(2,1)S(1)}, bf16[2,128,1,128]{3,1,0,2:T(8,128)(2,1)S(1)}, u32[]{:S(2)}, u32[]{:S(2)}) %collective-permute-start) | collective-permute-done | bytes 65568 | tf_op jit(solution)/shard_map/while/body/eval_jaxpr/ppermute | solution.py:17
  17.7 4.9 %collective-permute-done = bf16[2,128,1,128]{3,1,0,2:T(8,128)(2,1)S(1)} collective-permute-done((bf16[2,128,1,128]{3,1,0,2:T(8,128)(2,1)S(1)}, bf16[2,128,1,128]{3,1,0,2:T(8,128)(2,1)S(1)}, u32[]{:S(2)}, u32[]{:S(2)}) %collective-permute-start) | collective-permute-done | bytes 65568 | tf_op jit(solution)/shard_map/while/body/eval_jaxpr/ppermute | solution.py:17
  22.6 4.9 %collective-permute-done = bf16[2,128,1,128]{3,1,0,2:T(8,128)(2,1)S(1)} collective-permute-done((bf16[2,128,1,128]{3,1,0,2:T(8,128)(2,1)S(1)}, bf16[2,128,1,128]{3,1,0,2:T(8,128)(2,1)S(1)}, u32[]{:S(2)}, u32[]{:S(2)}) %collective-permute-start) | collective-permute-done | bytes 65568 | tf_op jit(solution)/shard_map/while/body/eval_jaxpr/ppermute | solution.py:17
  28.6 31.1 %while.124 = (s32[]{:T(128)}, bf16[8,128,1,8,128]{1,4,3,0,2:T(8,128)(2,1)S(1)}, f32[8,128,1,8]{1,3,2,0:T(8,128)}, s32[8,128]{1,0:T(8,128)S(1)}, bf16[8,128,1,8,1...) while((s32[]{:T(128)}, ...), condition=%wide.region_7.8_spmd.clone, body=%wide.region_4.7_spmd.clone.sunk | while | flops 272436736 | bytes 8837741 | solution.py:111
  32.7 1.5 fusion.114
  59.7 7.8 %all-to-all-start = ((f32[8,128,8]{1,2,0:T(8,128)}), f32[8,128,8]{1,2,0:T(8,128)S(1)}, u32[]{:S(2)}, u32[]{:S(2)}) async-start(f32[8,128,8]{1,2,0:T(8,128)} %bitcast.9), calls=%async_computation | async-start | bytes 65536 | tf_op jit(solution)/shard_map/all_to_all | solution.py:122
  67.5 3.9 %copy.84 = bf16[8,128,1024]{1,2,0:T(8,128)(2,1)} copy(bf16[8,128,1024]{2,1,0:T(8,128)(2,1)} %get-tuple-element.879) | data formatting | bytes 4194304
  71.5 15.4 %while.121 = (s32[]{:T(128)}, bf16[4,2,128,1,128]{4,2,0,3,1:T(8,128)(2,1)S(1)}, bf16[2,128,1,128]{3,1,0,2:T(8,128)(2,1)S(1)}, s32[]{:T(128)}, s32[]{:T(128)}, /*index=5*/s32[]{:T(128)}, s32[]{:T(128)}, s32[]{:T(128)}) while((s32[]{:T(128)}, bf16[4,2,128,1,128]{4,2,0,3,1:T(8,128)(2,1)S(1)}, bf16[2,128,1,128]{3,1,0,2:T(8,128)(2,1)S(1)}, ...), condition=%wide.region_12.13_spmd, body=%wide.region_11.12_spmd.sunk | while | flops 17 | bytes 524572 | solution.py:93
  71.6 5.4 %collective-permute-done.1 = bf16[2,128,1,128]{3,1,0,2:T(8,128)(2,1)S(1)} collective-permute-done((bf16[2,128,1,128]{3,1,0,2:T(8,128)(2,1)S(1)}, bf16[2,128,1,128]{3,1,0,2:T(8,128)(2,1)S(1)}, u32[]{:S(2)}, u32[]{:S(2)}) %collective-permute-start.1) | collective-permute-done | bytes 65568 | tf_op jit(solution)/shard_map/while/body/eval_jaxpr/ppermute | solution.py:17
  77.0 4.9 %collective-permute-done.1 = bf16[2,128,1,128]{3,1,0,2:T(8,128)(2,1)S(1)} collective-permute-done((bf16[2,128,1,128]{3,1,0,2:T(8,128)(2,1)S(1)}, bf16[2,128,1,128]{3,1,0,2:T(8,128)(2,1)S(1)}, u32[]{:S(2)}, u32[]{:S(2)}) %collective-permute-start.1) | collective-permute-done | bytes 65568 | tf_op jit(solution)/shard_map/while/body/eval_jaxpr/ppermute | solution.py:17
  82.0 4.9 %collective-permute-done.1 = bf16[2,128,1,128]{3,1,0,2:T(8,128)(2,1)S(1)} collective-permute-done((bf16[2,128,1,128]{3,1,0,2:T(8,128)(2,1)S(1)}, bf16[2,128,1,128]{3,1,0,2:T(8,128)(2,1)S(1)}, u32[]{:S(2)}, u32[]{:S(2)}) %collective-permute-start.1) | collective-permute-done | bytes 65568 | tf_op jit(solution)/shard_map/while/body/eval_jaxpr/ppermute | solution.py:17
  87.9 31.1 %while.125 = (s32[]{:T(128)}, bf16[8,128,1,8,128]{1,4,3,0,2:T(8,128)(2,1)S(1)}, f32[8,128,1,8]{1,3,2,0:T(8,128)}, s32[8,128]{1,0:T(8,128)S(1)}, bf16[8,128,1,8,1...) while((s32[]{:T(128)}, ...), condition=%wide.region_16.17_spmd.clone, body=%wide.region_13.16_spmd.clone.sunk | while | flops 272436736 | bytes 8837741 | solution.py:111
  95.9 1.5 fusion.122
  119.1 4.4 %copy.85 = bf16[8,128,1024]{1,2,0:T(8,128)(2,1)} copy(bf16[8,128,1024]{2,1,0:T(8,128)(2,1)} %get-tuple-element.878) | data formatting | bytes 4194304
  123.6 15.6 %while.122 = (s32[]{:T(128)}, bf16[4,2,128,1,128]{4,2,0,3,1:T(8,128)(2,1)S(1)}, bf16[2,128,1,128]{3,1,0,2:T(8,128)(2,1)S(1)}, s32[]{:T(128)}, s32[]{:T(128)}, /*index=5*/s32[]{:T(128)}, s32[]{:T(128)}, s32[]{:T(128)}) while((s32[]{:T(128)}, bf16[4,2,128,1,128]{4,2,0,3,1:T(8,128)(2,1)S(1)}, bf16[2,128,1,128]{3,1,0,2:T(8,128)(2,1)S(1)}, ...), condition=%wide.region_21.22_spmd, body=%wide.region_20.21_spmd.sunk | while | flops 17 | bytes 524572 | solution.py:93
  123.7 4.9 %collective-permute-done.2 = bf16[2,128,1,128]{3,1,0,2:T(8,128)(2,1)S(1)} collective-permute-done((bf16[2,128,1,128]{3,1,0,2:T(8,128)(2,1)S(1)}, bf16[2,128,1,128]{3,1,0,2:T(8,128)(2,1)S(1)}, u32[]{:S(2)}, u32[]{:S(2)}) %collective-permute-start.2) | collective-permute-done | bytes 65568 | tf_op jit(solution)/shard_map/while/body/eval_jaxpr/ppermute | solution.py:17
  128.6 4.9 %collective-permute-done.2 = bf16[2,128,1,128]{3,1,0,2:T(8,128)(2,1)S(1)} collective-permute-done((bf16[2,128,1,128]{3,1,0,2:T(8,128)(2,1)S(1)}, bf16[2,128,1,128]{3,1,0,2:T(8,128)(2,1)S(1)}, u32[]{:S(2)}, u32[]{:S(2)}) %collective-permute-start.2) | collective-permute-done | bytes 65568 | tf_op jit(solution)/shard_map/while/body/eval_jaxpr/ppermute | solution.py:17
  133.5 5.6 %collective-permute-done.2 = bf16[2,128,1,128]{3,1,0,2:T(8,128)(2,1)S(1)} collective-permute-done((bf16[2,128,1,128]{3,1,0,2:T(8,128)(2,1)S(1)}, bf16[2,128,1,128]{3,1,0,2:T(8,128)(2,1)S(1)}, u32[]{:S(2)}, u32[]{:S(2)}) %collective-permute-start.2) | collective-permute-done | bytes 65568 | tf_op jit(solution)/shard_map/while/body/eval_jaxpr/ppermute | solution.py:17
  140.3 31.2 %while.126 = (s32[]{:T(128)}, bf16[8,128,1,8,128]{1,4,3,0,2:T(8,128)(2,1)S(1)}, f32[8,128,1,8]{1,3,2,0:T(8,128)}, s32[8,128]{1,0:T(8,128)S(1)}, bf16[8,128,1,8,1...) while((s32[]{:T(128)}, ...), condition=%wide.region_25.26_spmd.clone, body=%wide.region_22.25_spmd.clone.sunk | while | flops 272436736 | bytes 8837741 | solution.py:111
  171.4 10.1 %all-to-all-start.2 = ((f32[8,128,8]{1,2,0:T(8,128)}), f32[8,128,8]{1,2,0:T(8,128)S(1)}, u32[]{:S(2)}, u32[]{:S(2)}) async-start(f32[8,128,8]{1,2,0:T(8,128)} %bitcast.17), calls=%async_computation.2 | async-start | bytes 65536 | tf_op jit(solution)/shard_map/all_to_all | solution.py:122
  181.6 15.4 %while.123 = (s32[]{:T(128)}, bf16[4,2,128,1,128]{4,2,0,3,1:T(8,128)(2,1)S(1)}, bf16[2,128,1,128]{3,1,0,2:T(8,128)(2,1)S(1)}, s32[]{:T(128)}, s32[]{:T(128)}, /*index=5*/s32[]{:T(128)}, s32[]{:T(128)}, s32[]{:T(128)}) while((s32[]{:T(128)}, bf16[4,2,128,1,128]{4,2,0,3,1:T(8,128)(2,1)S(1)}, bf16[2,128,1,128]{3,1,0,2:T(8,128)(2,1)S(1)}, ...), condition=%wide.region_30.31_spmd, body=%wide.region_29.30_spmd.sunk | while | flops 17 | bytes 524572 | solution.py:93
  181.7 5.4 %collective-permute-done.3 = bf16[2,128,1,128]{3,1,0,2:T(8,128)(2,1)S(1)} collective-permute-done((bf16[2,128,1,128]{3,1,0,2:T(8,128)(2,1)S(1)}, bf16[2,128,1,128]{3,1,0,2:T(8,128)(2,1)S(1)}, u32[]{:S(2)}, u32[]{:S(2)}) %collective-permute-start.3) | collective-permute-done | bytes 65568 | tf_op jit(solution)/shard_map/while/body/eval_jaxpr/ppermute | solution.py:17
  187.2 4.9 %collective-permute-done.3 = bf16[2,128,1,128]{3,1,0,2:T(8,128)(2,1)S(1)} collective-permute-done((bf16[2,128,1,128]{3,1,0,2:T(8,128)(2,1)S(1)}, bf16[2,128,1,128]{3,1,0,2:T(8,128)(2,1)S(1)}, u32[]{:S(2)}, u32[]{:S(2)}) %collective-permute-start.3) | collective-permute-done | bytes 65568 | tf_op jit(solution)/shard_map/while/body/eval_jaxpr/ppermute | solution.py:17
  192.1 4.9 %collective-permute-done.3 = bf16[2,128,1,128]{3,1,0,2:T(8,128)(2,1)S(1)} collective-permute-done((bf16[2,128,1,128]{3,1,0,2:T(8,128)(2,1)S(1)}, bf16[2,128,1,128]{3,1,0,2:T(8,128)(2,1)S(1)}, u32[]{:S(2)}, u32[]{:S(2)}) %collective-permute-start.3) | collective-permute-done | bytes 65568 | tf_op jit(solution)/shard_map/while/body/eval_jaxpr/ppermute | solution.py:17
  197.0 3.9 %copy.86 = bf16[8,128,1024]{1,2,0:T(8,128)(2,1)} copy(bf16[8,128,1024]{2,1,0:T(8,128)(2,1)} %get-tuple-element.880) | data formatting | bytes 4194304
  200.9 7.1 %all-to-all-start.4 = ((f32[8,128,8]{1,2,0:T(8,128)}), f32[8,128,8]{1,2,0:T(8,128)S(1)}, u32[]{:S(2)}, u32[]{:S(2)}) async-start(f32[8,128,8]{1,2,0:T(8,128)} %bitcast.25), calls=%async_computation.4 | async-start | bytes 65536 | tf_op jit(solution)/shard_map/all_to_all | solution.py:122
  208.5 26.6 %while.127 = (s32[]{:T(128)}, bf16[8,128,1,8,128]{1,4,3,0,2:T(8,128)(2,1)S(1)}, f32[8,128,1,8]{1,3,2,0:T(8,128)S(1)}, s32[8,128]{1,0:T(8,128)S(1)}, bf16[8,128,1...) while((s32[]{:T(128)}, ...), condition=%wide.region_34.35_spmd.clone, body=%wide.region_31.34_spmd.clone.sunk | while | flops 272436736 | bytes 8837233 | solution.py:111
  208.8 1.5 fusion.138
  212.1 1.5 fusion.138
  215.4 1.5 fusion.138
  218.7 1.5 fusion.138
  222.1 1.5 fusion.138
  225.4 1.5 fusion.138
  228.7 1.5 fusion.138
  232.1 1.5 fusion.138
  235.2 8.2 %all_to_all.40 = f32[8,128,8]{1,2,0:T(8,128)S(1)} all-to-all(f32[8,128,8]{1,2,0:T(8,128)S(1)} %bitcast.360), channel_id=1, replica_groups=mesh['row'=8,'col'=4] {'row'}, dimensions={0} | all-to-all | bytes 65536 | tf_op jit(solution)/shard_map/all_to_all | solution.py:122
  243.4 29.8 %all_to_all.41 = bf16[8,128,1024]{1,2,0:T(8,128)(2,1)S(1)} all-to-all(bf16[8,128,1024]{1,2,0:T(8,128)(2,1)} %bitcast.349), channel_id=1, replica_groups=mesh['row'=8,'col'=4] {'row'}, dimensions={0} | all-to-all | bytes 4194304 | tf_op jit(solution)/shard_map/all_to_all | solution.py:115
  273.2 29.7 %all_to_all.42 = bf16[8,128,1024]{1,2,0:T(8,128)(2,1)} all-to-all(bf16[8,128,1024]{1,2,0:T(8,128)(2,1)S(1)} %bitcast.350), channel_id=1, replica_groups=mesh['row'=8,'col'=4] {'row'}, dimensions={0} | all-to-all | bytes 4194304 | tf_op jit(solution)/shard_map/all_to_all | solution.py:115
  302.9 5.5 %all-to-all-start.5 = ((bf16[8,128,1024]{1,2,0:T(8,128)(2,1)}), bf16[8,128,1024]{1,2,0:T(8,128)(2,1)}, u32[]{:S(2)}, u32[]{:S(2)}) async-start(bf16[8,128,1024]{1,2,0:T(8,128)(2,1)} %bitcast.351), calls=%async_computation.5 | async-start | bytes 4194304 | tf_op jit(solution)/shard_map/all_to_all | solution.py:115
  308.5 23.0 %all-to-all-done.5 = bf16[8,128,1024]{1,2,0:T(8,128)(2,1)} async-done(((bf16[8,128,1024]{1,2,0:T(8,128)(2,1)}), bf16[8,128,1024]{1,2,0:T(8,128)(2,1)}, u32[]{:S(2)}, u32[]{:S(2)}) %all-to-all-start.5) | async-done | bytes 2097184 | tf_op jit(solution)/shard_map/all_to_all | solution.py:115
  331.5 7.8 %all-to-all-start.7 = ((bf16[8,128,1024]{1,2,0:T(8,128)(2,1)}), bf16[8,128,1024]{1,2,0:T(8,128)(2,1)}, u32[]{:S(2)}, u32[]{:S(2)}) async-start(bf16[8,128,1024]{1,2,0:T(8,128)(2,1)} %bitcast.348), calls=%async_computation.7 | async-start | bytes 4194304 | tf_op jit(solution)/shard_map/all_to_all | solution.py:115
  341.3 2.0 fusion.57
  343.4 19.1 %all-to-all-done.7 = bf16[8,128,1024]{1,2,0:T(8,128)(2,1)} async-done(((bf16[8,128,1024]{1,2,0:T(8,128)(2,1)}), bf16[8,128,1024]{1,2,0:T(8,128)(2,1)}, u32[]{:S(2)}, u32[]{:S(2)}) %all-to-all-start.7) | async-done | bytes 2097184 | tf_op jit(solution)/shard_map/all_to_all | solution.py:115
  362.5 2.0 fusion.56
  (471 shorter events, 114.1 us)
Async XLA Ops:
  11.8 5.8 %collective-permute-start = (bf16[2,128,1,128]{3,1,0,2:T(8,128)(2,1)S(1)}, bf16[2,128,1,128]{3,1,0,2:T(8,128)(2,1)S(1)}, u32[]{:S(2)}, u32[]{:S(2)}) collective-permute-start(bf16[2,128,1,128]{3,1,0,2:T(8,128)(2,1)S(1)} %copy.169), channel_id=1, source_target_pairs={{0,1},{1,2},{2,3},{3,0},{4,5},{5,6},{6,7},{7,4},{8,9},{9,10},{10,1... | collective-permute-start | bytes 196616 | tf_op jit(solution)/shard_map/while/body/eval_jaxpr/ppermute | solution.py:17
  17.6 4.9 %collective-permute-start = (bf16[2,128,1,128]{3,1,0,2:T(8,128)(2,1)S(1)}, bf16[2,128,1,128]{3,1,0,2:T(8,128)(2,1)S(1)}, u32[]{:S(2)}, u32[]{:S(2)}) collective-permute-start(bf16[2,128,1,128]{3,1,0,2:T(8,128)(2,1)S(1)} %copy.169), channel_id=1, source_target_pairs={{0,1},{1,2},{2,3},{3,0},{4,5},{5,6},{6,7},{7,4},{8,9},{9,10},{10,1... | collective-permute-start | bytes 196616 | tf_op jit(solution)/shard_map/while/body/eval_jaxpr/ppermute | solution.py:17
  22.6 4.9 %collective-permute-start = (bf16[2,128,1,128]{3,1,0,2:T(8,128)(2,1)S(1)}, bf16[2,128,1,128]{3,1,0,2:T(8,128)(2,1)S(1)}, u32[]{:S(2)}, u32[]{:S(2)}) collective-permute-start(bf16[2,128,1,128]{3,1,0,2:T(8,128)(2,1)S(1)} %copy.169), channel_id=1, source_target_pairs={{0,1},{1,2},{2,3},{3,0},{4,5},{5,6},{6,7},{7,4},{8,9},{9,10},{10,1... | collective-permute-start | bytes 196616 | tf_op jit(solution)/shard_map/while/body/eval_jaxpr/ppermute | solution.py:17
  59.7 11.7 %copy-start.2 = (bf16[8,128,1,8,128]{1,4,3,0,2:T(8,128)(2,1)}, bf16[8,128,1,8,128]{1,4,3,0,2:T(8,128)(2,1)S(1)}, u32[]{:S(2)}) copy-start(bf16[8,128,1,8,128]{1,4,3,0,2:T(8,128)(2,1)S(1)} %get-tuple-element.608) | copy-start | bytes 6291460
  59.7 111.7 %all-to-all-start = ((f32[8,128,8]{1,2,0:T(8,128)}), f32[8,128,8]{1,2,0:T(8,128)S(1)}, u32[]{:S(2)}, u32[]{:S(2)}) async-start(f32[8,128,8]{1,2,0:T(8,128)} %bitcast.9), calls=%async_computation | async-start | bytes 65536 | tf_op jit(solution)/shard_map/all_to_all | solution.py:122
  71.5 5.5 %collective-permute-start.1 = (bf16[2,128,1,128]{3,1,0,2:T(8,128)(2,1)S(1)}, bf16[2,128,1,128]{3,1,0,2:T(8,128)(2,1)S(1)}, u32[]{:S(2)}, u32[]{:S(2)}) collective-permute-start(bf16[2,128,1,128]{3,1,0,2:T(8,128)(2,1)S(1)} %copy.150), channel_id=1, source_target_pairs={{0,1},{1,2},{2,3},{3,0},{4,5},{5,6},{6,7},{7,4},{8,9},{9,10},{10,1... | collective-permute-start | bytes 196616 | tf_op jit(solution)/shard_map/while/body/eval_jaxpr/ppermute | solution.py:17
  77.0 4.9 %collective-permute-start.1 = (bf16[2,128,1,128]{3,1,0,2:T(8,128)(2,1)S(1)}, bf16[2,128,1,128]{3,1,0,2:T(8,128)(2,1)S(1)}, u32[]{:S(2)}, u32[]{:S(2)}) collective-permute-start(bf16[2,128,1,128]{3,1,0,2:T(8,128)(2,1)S(1)} %copy.150), channel_id=1, source_target_pairs={{0,1},{1,2},{2,3},{3,0},{4,5},{5,6},{6,7},{7,4},{8,9},{9,10},{10,1... | collective-permute-start | bytes 196616 | tf_op jit(solution)/shard_map/while/body/eval_jaxpr/ppermute | solution.py:17
  81.9 4.9 %collective-permute-start.1 = (bf16[2,128,1,128]{3,1,0,2:T(8,128)(2,1)S(1)}, bf16[2,128,1,128]{3,1,0,2:T(8,128)(2,1)S(1)}, u32[]{:S(2)}, u32[]{:S(2)}) collective-permute-start(bf16[2,128,1,128]{3,1,0,2:T(8,128)(2,1)S(1)} %copy.150), channel_id=1, source_target_pairs={{0,1},{1,2},{2,3},{3,0},{4,5},{5,6},{6,7},{7,4},{8,9},{9,10},{10,1... | collective-permute-start | bytes 196616 | tf_op jit(solution)/shard_map/while/body/eval_jaxpr/ppermute | solution.py:17
  119.1 4.4 %copy-start.3 = (bf16[8,128,1,8,128]{1,4,3,0,2:T(8,128)(2,1)}, bf16[8,128,1,8,128]{1,4,3,0,2:T(8,128)(2,1)S(1)}, u32[]{:S(2)}) copy-start(bf16[8,128,1,8,128]{1,4,3,0,2:T(8,128)(2,1)S(1)} %get-tuple-element.612) | copy-start | bytes 6291460
  123.6 5.0 %collective-permute-start.2 = (bf16[2,128,1,128]{3,1,0,2:T(8,128)(2,1)S(1)}, bf16[2,128,1,128]{3,1,0,2:T(8,128)(2,1)S(1)}, u32[]{:S(2)}, u32[]{:S(2)}) collective-permute-start(bf16[2,128,1,128]{3,1,0,2:T(8,128)(2,1)S(1)} %copy.131), channel_id=1, source_target_pairs={{0,1},{1,2},{2,3},{3,0},{4,5},{5,6},{6,7},{7,4},{8,9},{9,10},{10,1... | collective-permute-start | bytes 196616 | tf_op jit(solution)/shard_map/while/body/eval_jaxpr/ppermute | solution.py:17
  128.6 4.9 %collective-permute-start.2 = (bf16[2,128,1,128]{3,1,0,2:T(8,128)(2,1)S(1)}, bf16[2,128,1,128]{3,1,0,2:T(8,128)(2,1)S(1)}, u32[]{:S(2)}, u32[]{:S(2)}) collective-permute-start(bf16[2,128,1,128]{3,1,0,2:T(8,128)(2,1)S(1)} %copy.131), channel_id=1, source_target_pairs={{0,1},{1,2},{2,3},{3,0},{4,5},{5,6},{6,7},{7,4},{8,9},{9,10},{10,1... | collective-permute-start | bytes 196616 | tf_op jit(solution)/shard_map/while/body/eval_jaxpr/ppermute | solution.py:17
  133.5 5.6 %collective-permute-start.2 = (bf16[2,128,1,128]{3,1,0,2:T(8,128)(2,1)S(1)}, bf16[2,128,1,128]{3,1,0,2:T(8,128)(2,1)S(1)}, u32[]{:S(2)}, u32[]{:S(2)}) collective-permute-start(bf16[2,128,1,128]{3,1,0,2:T(8,128)(2,1)S(1)} %copy.131), channel_id=1, source_target_pairs={{0,1},{1,2},{2,3},{3,0},{4,5},{5,6},{6,7},{7,4},{8,9},{9,10},{10,1... | collective-permute-start | bytes 196616 | tf_op jit(solution)/shard_map/while/body/eval_jaxpr/ppermute | solution.py:17
  171.4 29.4 %copy-start.5 = (bf16[8,128,1,8,128]{1,4,3,0,2:T(8,128)(2,1)}, bf16[8,128,1,8,128]{1,4,3,0,2:T(8,128)(2,1)S(1)}, u32[]{:S(2)}) copy-start(bf16[8,128,1,8,128]{1,4,3,0,2:T(8,128)(2,1)S(1)} %get-tuple-element.616) | copy-start | bytes 6291460
  171.4 29.4 %all-to-all-start.2 = ((f32[8,128,8]{1,2,0:T(8,128)}), f32[8,128,8]{1,2,0:T(8,128)S(1)}, u32[]{:S(2)}, u32[]{:S(2)}) async-start(f32[8,128,8]{1,2,0:T(8,128)} %bitcast.17), calls=%async_computation.2 | async-start | bytes 65536 | tf_op jit(solution)/shard_map/all_to_all | solution.py:122
  181.6 5.5 %collective-permute-start.3 = (bf16[2,128,1,128]{3,1,0,2:T(8,128)(2,1)S(1)}, bf16[2,128,1,128]{3,1,0,2:T(8,128)(2,1)S(1)}, u32[]{:S(2)}, u32[]{:S(2)}) collective-permute-start(bf16[2,128,1,128]{3,1,0,2:T(8,128)(2,1)S(1)} %copy.112), channel_id=1, source_target_pairs={{0,1},{1,2},{2,3},{3,0},{4,5},{5,6},{6,7},{7,4},{8,9},{9,10},{10,1... | collective-permute-start | bytes 196616 | tf_op jit(solution)/shard_map/while/body/eval_jaxpr/ppermute | solution.py:17
  187.1 4.9 %collective-permute-start.3 = (bf16[2,128,1,128]{3,1,0,2:T(8,128)(2,1)S(1)}, bf16[2,128,1,128]{3,1,0,2:T(8,128)(2,1)S(1)}, u32[]{:S(2)}, u32[]{:S(2)}) collective-permute-start(bf16[2,128,1,128]{3,1,0,2:T(8,128)(2,1)S(1)} %copy.112), channel_id=1, source_target_pairs={{0,1},{1,2},{2,3},{3,0},{4,5},{5,6},{6,7},{7,4},{8,9},{9,10},{10,1... | collective-permute-start | bytes 196616 | tf_op jit(solution)/shard_map/while/body/eval_jaxpr/ppermute | solution.py:17
  192.0 4.9 %collective-permute-start.3 = (bf16[2,128,1,128]{3,1,0,2:T(8,128)(2,1)S(1)}, bf16[2,128,1,128]{3,1,0,2:T(8,128)(2,1)S(1)}, u32[]{:S(2)}, u32[]{:S(2)}) collective-permute-start(bf16[2,128,1,128]{3,1,0,2:T(8,128)(2,1)S(1)} %copy.112), channel_id=1, source_target_pairs={{0,1},{1,2},{2,3},{3,0},{4,5},{5,6},{6,7},{7,4},{8,9},{9,10},{10,1... | collective-permute-start | bytes 196616 | tf_op jit(solution)/shard_map/while/body/eval_jaxpr/ppermute | solution.py:17
  200.9 34.3 %all-to-all-start.4 = ((f32[8,128,8]{1,2,0:T(8,128)}), f32[8,128,8]{1,2,0:T(8,128)S(1)}, u32[]{:S(2)}, u32[]{:S(2)}) async-start(f32[8,128,8]{1,2,0:T(8,128)} %bitcast.25), calls=%async_computation.4 | async-start | bytes 65536 | tf_op jit(solution)/shard_map/all_to_all | solution.py:122
  235.1 8.3 %copy-start.1 = (bf16[8,128,1,8,128]{1,4,3,0,2:T(8,128)(2,1)}, bf16[8,128,1,8,128]{1,4,3,0,2:T(8,128)(2,1)S(1)}, u32[]{:S(2)}) copy-start(bf16[8,128,1,8,128]{1,4,3,0,2:T(8,128)(2,1)S(1)} %get-tuple-element.620) | copy-start | bytes 6291460
  243.4 29.8 %copy-start.4 = (bf16[8,128,1,8,128]{1,4,3,0,2:T(8,128)(2,1)S(1)}, bf16[8,128,1,8,128]{1,4,3,0,2:T(8,128)(2,1)}, u32[]{:S(2)}) copy-start(bf16[8,128,1,8,128]{1,4,3,0,2:T(8,128)(2,1)} %copy-done.3) | copy-start | bytes 6291460
  302.9 28.6 %all-to-all-start.5 = ((bf16[8,128,1024]{1,2,0:T(8,128)(2,1)}), bf16[8,128,1024]{1,2,0:T(8,128)(2,1)}, u32[]{:S(2)}, u32[]{:S(2)}) async-start(bf16[8,128,1024]{1,2,0:T(8,128)(2,1)} %bitcast.351), calls=%async_computation.5 | async-start | bytes 4194304 | tf_op jit(solution)/shard_map/all_to_all | solution.py:115
  331.5 31.0 %all-to-all-start.7 = ((bf16[8,128,1024]{1,2,0:T(8,128)(2,1)}), bf16[8,128,1024]{1,2,0:T(8,128)(2,1)}, u32[]{:S(2)}, u32[]{:S(2)}) async-start(bf16[8,128,1024]{1,2,0:T(8,128)(2,1)} %bitcast.348), calls=%async_computation.7 | async-start | bytes 4194304 | tf_op jit(solution)/shard_map/all_to_all | solution.py:115
  339.3 1.6 copy-start
where the time goes:
time: 372 us; the launch traced here: 366 us
  waiting for transfers between devices  101 us (27%)
  matrix products  68.2 us (18%)
  blocking collectives  67.7 us (18%)
  other arithmetic  49 us (13%)
  starting transfers between devices  40.7 us (11%)
  local copies, waits for them, and re-layouts  36.6 us (10%)
    all_to_all x2, blocking collectives, shards(): lax.all_to_all(partial_value.reshape(rows, block_rows, group * HEAD_DIM),...  59.5 us
    ppermute x12, waiting for transfers between devices, passed_along(): return lax.ppermute(value, axis, pairs)  58.9 us
    dot_general x32, matrix products, attend(): jnp.einsum('nkgd,skd->nkgs', queries, keys, preferred_element_type=jnp.fl...  48.9 us
    all_to_all x2, waiting for transfers between devices, shards(): lax.all_to_all(partial_value.reshape(rows, block_rows, group * HEAD_DIM),...  42.1 us
    all_to_all x3, starting transfers between devices, shards(): lax.all_to_all(log_sum.reshape(rows, block_rows, group), 'row', split_axi...  25 us
    reduce_sum x32, other arithmetic, attend(): total = jnp.sum(raised, axis=-1)  21.5 us
    dot_general x32, matrix products, attend(): jnp.einsum('nkgs,skd->nkgd', weights, values, preferred_element_type=jnp....  19.3 us
    unnamed x16, local copies, waits for them, and re-layouts  15.7 us
  transfers between devices with their start and end apart: 17, of which 14 were waited for; matrix products, arithmetic and copies ran while one was open for 29% of the time, Pallas kernels for 0%

commit v1 on v0

v1 whole, which is shorter than its diff:
```python
import functools
import math

import jax
import jax.numpy as jnp
from jax import lax
from jax.experimental import pallas as pl
from jax.experimental.pallas import tpu as pltpu
from jax.sharding import PartitionSpec as P

HEAD_DIM = 128
QHEADS = 32
KVHEADS = 4
GROUP = QHEADS // KVHEADS
masked_score = -1e30
MESH = pl.DeviceIdType.MESH
VMEM_LIMIT = 60 * 1024 * 1024


def device(row, col):
    return {"row": row, "col": col}


def spread_kernel(rows, cols, key_ref, value_ref, out_ref, held, own_sem, plane_send, plane_recv,
                  col_send, col_recv, side_send, side_recv, out_sem):
    share = rows // KVHEADS
    row, col = lax.axis_index("row"), lax.axis_index("col")
    head, lane = row // share, row % share
    peers = []
    for step in range(1, KVHEADS):
        peers.append((lax.rem(head + step, KVHEADS) * share + lane, col))
    for step in range(1, cols):
        peers.append((row, lax.rem(col + step, cols)))
    for step in range(1, share):
        peers.append((head * share + lax.rem(lane + step, share), col))
    barrier = pltpu.get_barrier_semaphore()
    for peer in peers:
        pl.semaphore_signal(barrier, inc=1, device_id=device(*peer), device_id_type=MESH)
    pl.semaphore_wait(barrier, len(peers))

    sent = []
    plane = []
    for step in range(1, KVHEADS):
        other = lax.rem(head + step, KVHEADS)
        columns = pl.ds(pl.multiple_of(other * HEAD_DIM, HEAD_DIM), HEAD_DIM)
        for kind, ref in enumerate((key_ref, value_ref)):
            copy = pltpu.make_async_remote_copy(
                src_ref=ref.at[:, columns],
                dst_ref=held.at[col, lane, head, kind],
                send_sem=plane_send.at[step - 1, kind],
                recv_sem=plane_recv.at[step - 1, kind],
                device_id=device(other * share + lane, col),
                device_id_type=MESH,
            )
            copy.start()
            plane.append(copy)
    columns = pl.ds(pl.multiple_of(head * HEAD_DIM, HEAD_DIM), HEAD_DIM)
    own = []
    for kind, ref in enumerate((key_ref, value_ref)):
        copy = pltpu.make_async_copy(ref.at[:, columns], held.at[col, lane, head, kind], own_sem.at[kind])
        copy.start()
        own.append(copy)
    for copy in own:
        copy.wait()
    for copy in plane:
        copy.wait_recv()
    sent += plane
    along = []
    for step in range(1, cols):
        copy = pltpu.make_async_remote_copy(
            src_ref=held.at[col, lane],
            dst_ref=held.at[col, lane],
            send_sem=col_send.at[step - 1],
            recv_sem=col_recv.at[step - 1],
            device_id=device(row, lax.rem(col + step, cols)),
            device_id_type=MESH,
        )
        copy.start()
        along.append(copy)
    sent += along
    stores = []
    side = []
    for step in range(cols):
        source = lax.rem(col - step + cols, cols)
        if step:
            along[step - 1].wait_recv()
        for other in range(1, share):
            copy = pltpu.make_async_remote_copy(
                src_ref=held.at[source, lane],
                dst_ref=held.at[source, lane],
                send_sem=side_send.at[step, other - 1],
                recv_sem=side_recv.at[step, other - 1],
                device_id=device(head * share + lax.rem(lane + other, share), col),
                device_id_type=MESH,
            )
            copy.start()
            side.append((copy, source, other, step))
        store = pltpu.make_async_copy(held.at[source, lane], out_ref.at[source, lane], out_sem.at[step, 0])
        store.start()
        stores.append(store)
    for copy, source, other, step in side:
        copy.wait_recv()
        there = lax.rem(lane - other + share, share)
        store = pltpu.make_async_copy(held.at[source, there], out_ref.at[source, there], out_sem.at[step, other])
        store.start()
        stores.append(store)
        sent.append(copy)
    for copy in sent:
        copy.wait_send()
    for store in stores:
        store.wait()


def spread(key, value, rows, cols):
    share = rows // KVHEADS
    tokens = key.shape[0]
    shape = (cols, share, KVHEADS, 2, tokens, HEAD_DIM)
    dma = pltpu.SemaphoreType.DMA
    return pl.pallas_call(
        functools.partial(spread_kernel, rows, cols),
        out_shape=jax.ShapeDtypeStruct(shape, key.dtype),
        in_specs=[pl.BlockSpec(memory_space=pltpu.VMEM)] * 2,
        out_specs=pl.BlockSpec(memory_space=pl.ANY),
        scratch_shapes=[
            pltpu.VMEM(shape, key.dtype),
            dma((2,)),
            dma((KVHEADS - 1, 2)),
            dma((KVHEADS - 1, 2)),
            dma((cols - 1,)),
            dma((cols - 1,)),
            dma((cols, share - 1)),
            dma((cols, share - 1)),
            dma((cols, share)),
        ],
        compiler_params=pltpu.CompilerParams(
            collective_id=0, has_side_effects=True, vmem_limit_bytes=VMEM_LIMIT
        ),
        name="spread",
    )(key, value)


def attend_kernel(cols, share, chunk_spans, order_ref, place_ref, query_ref, held_ref, out_ref,
                  keys, values, queries, best, total):
    tokens = query_ref.shape[1]
    heads = query_ref.shape[2] // HEAD_DIM
    count = heads * tokens
    spans = order_ref.shape[0]
    step = pl.program_id(0)
    width = chunk_spans * tokens

    @pl.when(step == 0)
    def _():
        values[:, HEAD_DIM:] = jnp.ones((values.shape[0], HEAD_DIM), values.dtype)

        def place(span, carry):
            row, col = span // cols, span % cols
            spot = pl.ds(pl.multiple_of(order_ref[span] * tokens, tokens), tokens)
            block = held_ref[col, row % share, row // share, 0]
            keys[spot, :HEAD_DIM] = block
            keys[spot, HEAD_DIM:] = block
            values[spot, :HEAD_DIM] = held_ref[col, row % share, row // share, 1]
            return carry

        lax.fori_loop(0, spans, place, 0)

    scale = math.log2(math.e) / math.sqrt(HEAD_DIM)
    for head in range(heads):
        part = query_ref[0, :, head * HEAD_DIM : (head + 1) * HEAD_DIM].astype(jnp.float32) * scale
        high = part.astype(jnp.bfloat16)
        low = (part - high.astype(jnp.float32)).astype(jnp.bfloat16)
        queries[head * tokens : (head + 1) * tokens, :HEAD_DIM] = high
        queries[head * tokens : (head + 1) * tokens, HEAD_DIM:] = low

    mine = order_ref[step * cols + place_ref[1]]
    last = mine // chunk_spans
    strip = 2 * tokens if heads % 2 == 0 else tokens

    def chunk(index, first):
        spot = pl.ds(pl.multiple_of(index * width, width), width)
        for start in range(0, count, strip):
            lines = slice(start, start + strip)
            scores = lax.dot_general(
                queries[lines, :], keys[spot, :], (((1,), (1,)), ((), ())), preferred_element_type=jnp.float32
            )
            if first:
                below = lax.broadcasted_iota(jnp.int32, scores.shape, 0) % tokens
                across = lax.broadcasted_iota(jnp.int32, scores.shape, 1)
                scores = jnp.where(across <= below + (mine % chunk_spans) * tokens, scores, masked_score)
                newest = jnp.max(scores, axis=1, keepdims=True)
            else:
                before = best[lines, :1]
                newest = jnp.maximum(before, jnp.max(scores, axis=1, keepdims=True))
            raised = jnp.exp2(scores - newest).astype(jnp.bfloat16)
            update = jnp.dot(raised, values[spot, :], preferred_element_type=jnp.float32)
            if first:
                total[lines, :] = update
            else:
                total[lines, :] = total[lines, :] * jnp.exp2(before - newest) + update
            best[lines, :] = jnp.broadcast_to(newest, (strip, HEAD_DIM))

    chunk(last, True)

    def body(index, carry):
        chunk(index, False)
        return carry

    lax.fori_loop(0, last, body, 0)
    for head in range(heads):
        lines = slice(head * tokens, (head + 1) * tokens)
        out_ref[0, :, head * HEAD_DIM : (head + 1) * HEAD_DIM] = (
            total[lines, :HEAD_DIM] / total[lines, HEAD_DIM:]
        ).astype(out_ref.dtype)


def attend(query, held, span_order, rows, cols):
    share = rows // KVHEADS
    tokens = query.shape[1]
    width = query.shape[2] // rows
    spans = span_order.shape[0]
    sequence = spans * tokens
    count = width // HEAD_DIM * tokens
    chunk_spans = 4
    place = jnp.stack([lax.axis_index("row"), lax.axis_index("col")]).astype(jnp.int32)
    return pl.pallas_call(
        functools.partial(attend_kernel, cols, share, chunk_spans),
        out_shape=jax.ShapeDtypeStruct((rows, tokens, width), query.dtype),
        grid_spec=pltpu.PrefetchScalarGridSpec(
            num_scalar_prefetch=2,
            grid=(rows,),
            in_specs=[
                pl.BlockSpec((1, tokens, width), lambda step, order, place: (step, 0, place[0])),
                pl.BlockSpec(held.shape, lambda step, order, place: (0,) * held.ndim),
            ],
            out_specs=pl.BlockSpec((1, tokens, width), lambda step, order, place: (step, 0, 0)),
            scratch_shapes=[
                pltpu.VMEM((sequence, 2 * HEAD_DIM), jnp.bfloat16),
                pltpu.VMEM((sequence, 2 * HEAD_DIM), jnp.bfloat16),
                pltpu.VMEM((count, 2 * HEAD_DIM), jnp.bfloat16),
                pltpu.VMEM((count, HEAD_DIM), jnp.float32),
                pltpu.VMEM((count, 2 * HEAD_DIM), jnp.float32),
            ],
        ),
        compiler_params=pltpu.CompilerParams(
            dimension_semantics=("arbitrary",), vmem_limit_bytes=VMEM_LIMIT
        ),
        name="attend",
    )(span_order, place, query, held)


def deliver_kernel(rows, part_ref, out_ref, own_sem, send_sem, recv_sem):
    row, col = lax.axis_index("row"), lax.axis_index("col")
    width = part_ref.shape[2]
    barrier = pltpu.get_barrier_semaphore()
    for step in range(1, rows):
        pl.semaphore_signal(
            barrier, inc=1, device_id=device(lax.rem(row + step, rows), col), device_id_type=MESH
        )
    pl.semaphore_wait(barrier, rows - 1)
    columns = pl.ds(pl.multiple_of(row * width, width), width)
    copies = []
    for step in range(1, rows):
        target = lax.rem(row + step, rows)
        copy = pltpu.make_async_remote_copy(
            src_ref=part_ref.at[target],
            dst_ref=out_ref.at[:, columns],
            send_sem=send_sem.at[step - 1],
            recv_sem=recv_sem.at[step - 1],
            device_id=device(target, col),
            device_id_type=MESH,
        )
        copy.start()
        copies.append(copy)
    own = pltpu.make_async_copy(part_ref.at[row], out_ref.at[:, columns], own_sem)
    own.start()
    own.wait()
    for copy in copies:
        copy.wait()


def deliver(parts):
    rows, tokens, width = parts.shape
    dma = pltpu.SemaphoreType.DMA
    return pl.pallas_call(
        functools.partial(deliver_kernel, rows),
        out_shape=jax.ShapeDtypeStruct((tokens, rows * width), parts.dtype),
        in_specs=[pl.BlockSpec(memory_space=pltpu.VMEM)],
        out_specs=pl.BlockSpec(memory_space=pl.ANY),
        scratch_shapes=[dma(()), dma((rows - 1,)), dma((rows - 1,))],
        compiler_params=pltpu.CompilerParams(
            collective_id=1, has_side_effects=True, vmem_limit_bytes=VMEM_LIMIT
        ),
        name="deliver",
    )(parts)


def shards(query, key, value, span_order):
    rows = lax.axis_size("row")
    cols = lax.axis_size("col")
    held = spread(key, value, rows, cols)
    parts = attend(query, held, span_order, rows, cols)
    return deliver(parts)


def solution(mesh):
    placed = (P(None, "col", None), P(("row", "col"), None), P(("row", "col"), None), P())
    return jax.shard_map(
        shards, mesh=mesh, in_specs=placed, out_specs=P(("row", "col"), None), check_vma=False
    )
```

time: 372 us -> 93.8 us (0.25)
  the two profiles are of different devices: /device:TPU:1 before, /device:TPU:9 now
where the time goes in v1:
time: 93.8 us; the launch traced here: 93.1 us
  Pallas kernels  90.2 us (96%)
  local copies, waits for them, and re-layouts  2.29 us (2%)
    pallas_call x1, Pallas kernels, attend(): pl.pallas_call(functools.partial(attend_kernel, cols, share, chunk_spans)...  39.6 us
    pallas_call x1, Pallas kernels, spread(): pl.pallas_call(functools.partial(spread_kernel, rows, cols), out_shape=ja...  33.9 us
    pallas_call x1, Pallas kernels, deliver(): pl.pallas_call(functools.partial(deliver_kernel, rows), out_shape=jax.Sha...  16.7 us
    unnamed x1, local copies, waits for them, and re-layouts  2.29 us

profile of v1, /device:TPU:9, one launch (start us, length us, event | category | flops | bytes accessed | tf_op | source)
XLA Modules:
  0.0 93.1 jit_solution(9364035491554548217)
XLA Ops:
  0.0 0.6 pad_add_fusion.place_ref
  0.6 33.9 %spread.1.held_ref = bf16[4,2,4,2,128,128]{5,4,3,2,1,0:T(8,128)(2,1)} custom-call(bf16[128,512]{1,0:T(8,128)(2,1)} %key_ref.1, bf16[128,512]{1,0:T(8,128)(2,1)} %value_ref.1), custom_call_target="tpu_custom_call" | custom-call | tf_op jit(solution)/shard_map/spread/pallas_call | solution.py:119
  34.5 39.6 %attend.1.part_ref = bf16[8,128,512]{2,1,0:T(8,128)(2,1)} custom-call(s32[32]{0:T(128)} %order_ref.1, s32[2]{0:T(128)} %pad_add_fusion.place_ref, bf16[8,128,4096]{2,1,0:T(8,128)(2,1)} %query_ref.1, bf16[4,2,4,2,128,128]{5,4,3,2,1,0:T(8,128)(2,1)} %spread.1.held_ref), custom_call_target="tpu_custom_call" | custom-call | tf_op jit(solution)/shard_map/attend/pallas_call | solution.py:224
  74.1 16.7 %deliver.1 = bf16[128,4096]{1,0:T(8,128)(2,1)} custom-call(bf16[8,128,512]{2,1,0:T(8,128)(2,1)} %attend.1.part_ref), custom_call_target="tpu_custom_call" | custom-call | tf_op jit(solution)/shard_map/deliver/pallas_call | solution.py:283
  90.8 2.3 %copy.6 = bf16[128,4096]{1,0:T(8,128)(2,1)} copy(bf16[128,4096]{1,0:T(8,128)(2,1)} %deliver.1) | data formatting | bytes 2097152

commit v2 on v1

--- a/solution.py
+++ b/solution.py
@@ -26,19 +26,22 @@
     share = rows // KVHEADS
     row, col = lax.axis_index("row"), lax.axis_index("col")
     head, lane = row // share, row % share
-    peers = []
-    for step in range(1, KVHEADS):
-        peers.append((lax.rem(head + step, KVHEADS) * share + lane, col))
-    for step in range(1, cols):
-        peers.append((row, lax.rem(col + step, cols)))
-    for step in range(1, share):
-        peers.append((head * share + lax.rem(lane + step, share), col))
     barrier = pltpu.get_barrier_semaphore()
+    peers = [(lax.rem(head + step, KVHEADS) * share + lane, col) for step in range(1, KVHEADS)]
+    peers += [(head * share + lax.rem(lane + step, share), col) for step in range(1, share)]
     for peer in peers:
         pl.semaphore_signal(barrier, inc=1, device_id=device(*peer), device_id_type=MESH)
-    pl.semaphore_wait(barrier, len(peers))
-
-    sent = []
+    ways = (1, -1)
+    for way in ways:
+        beside = jnp.logical_and(col + way >= 0, col + way < cols)
+
+        @pl.when(beside)
+        def _(way=way):
+            pl.semaphore_signal(barrier, inc=1, device_id=device(row, col + way), device_id_type=MESH)
+
+    ends = jnp.where(col == 0, 1, 0) + jnp.where(col == cols - 1, 1, 0)
+    pl.semaphore_wait(barrier, len(peers) + len(ways) - ends)
+
     plane = []
     for step in range(1, KVHEADS):
         other = lax.rem(head + step, KVHEADS)
@@ -62,53 +65,118 @@
         own.append(copy)
     for copy in own:
         copy.wait()
+
+    def slot_of(piece):
+        return lax.rem(head - piece + KVHEADS, KVHEADS)
+
+    def source_of(step, way):
+        return col - way * step
+
+    def way_index(way):
+        return ways.index(way)
+
+    def held_here(step, way):
+        source = source_of(step, way)
+        return jnp.logical_and(source >= 0, source < cols)
+
+    def passes_on(step, way):
+        target = col + way
+        return jnp.logical_and(held_here(step, way), jnp.logical_and(target >= 0, target < cols))
+
+    def on_copy(step, way, piece):
+        spot = held.at[source_of(step, way), lane, slot_of(piece)]
+        return pltpu.make_async_remote_copy(
+            src_ref=spot,
+            dst_ref=spot,
+            send_sem=col_send.at[step, way_index(way), piece],
+            recv_sem=col_recv.at[step, way_index(way), piece],
+            device_id=device(row, col + way),
+            device_id_type=MESH,
+        )
+
+    def in_copy(step, way, piece):
+        spot = held.at[source_of(step + 1, way), lane, slot_of(piece)]
+        return pltpu.make_async_remote_copy(
+            src_ref=spot,
+            dst_ref=spot,
+            send_sem=col_send.at[step, way_index(way), piece],
+            recv_sem=col_recv.at[step, way_index(way), piece],
+            device_id=device(row, col - way),
+            device_id_type=MESH,
+        )
+
+    def side_copy(step, way, piece, other, arriving):
+        there = lax.rem(lane - other + share, share) if arriving else lane
+        spot = held.at[source_of(step, way), there, slot_of(piece)]
+        return pltpu.make_async_remote_copy(
+            src_ref=spot,
+            dst_ref=spot,
+            send_sem=side_send.at[step, way_index(way), piece, other - 1],
+            recv_sem=side_recv.at[step, way_index(way), piece, other - 1],
+            device_id=device(head * share + lax.rem(lane + other, share), col),
+            device_id_type=MESH,
+        )
+
+    def out_copy(step, way, other):
+        there = lax.rem(lane - other + share, share)
+        source = source_of(step, way)
+        return pltpu.make_async_copy(
+            held.at[source, there], out_ref.at[source, there], out_sem.at[step, way_index(way), other]
+        )
+
+    def store(step):
+        for way in ways if step else (1,):
+            @pl.when(held_here(step, way))
+            def _(way=way):
+                for other in range(share):
+                    if other:
+                        for piece in range(KVHEADS):
+                            side_copy(step, way, piece, other, True).wait_recv()
+                    out_copy(step, way, other).start()
+
+    for step in range(cols):
+        for piece in range(KVHEADS):
+            if step == 0 and piece:
+                for copy in plane[2 * (piece - 1) : 2 * piece]:
+                    copy.wait_recv()
+            for way in ways:
+                if step:
+                    @pl.when(held_here(step, way))
+                    def _(way=way):
+                        in_copy(step - 1, way, piece).wait_recv()
+
+                if step < cols - 1:
+                    @pl.when(passes_on(step, way))
+                    def _(way=way):
+                        on_copy(step, way, piece).start()
+
+                if step or way == 1:
+                    @pl.when(held_here(step, way))
+                    def _(way=way):
+                        for other in range(1, share):
+                            side_copy(step, way, piece, other, False).start()
+
+        if step:
+            store(step - 1)
+    store(cols - 1)
     for copy in plane:
-        copy.wait_recv()
-    sent += plane
-    along = []
-    for step in range(1, cols):
-        copy = pltpu.make_async_remote_copy(
-            src_ref=held.at[col, lane],
-            dst_ref=held.at[col, lane],
-            send_sem=col_send.at[step - 1],
-            recv_sem=col_recv.at[step - 1],
-            device_id=device(row, lax.rem(col + step, cols)),
-            device_id_type=MESH,
-        )
-        copy.start()
-        along.append(copy)
-    sent += along
-    stores = []
-    side = []
+        copy.wait_send()
     for step in range(cols):
-        source = lax.rem(col - step + cols, cols)
-        if step:
-            along[step - 1].wait_recv()
-        for other in range(1, share):
-            copy = pltpu.make_async_remote_copy(
-                src_ref=held.at[source, lane],
-                dst_ref=held.at[source, lane],
-                send_sem=side_send.at[step, other - 1],
-                recv_sem=side_recv.at[step, other - 1],
-                device_id=device(head * share + lax.rem(lane + other, share), col),
-                device_id_type=MESH,
-            )
-            copy.start()
-            side.append((copy, source, other, step))
-        store = pltpu.make_async_copy(held.at[source, lane], out_ref.at[source, lane], out_sem.at[step, 0])
-        store.start()
-        stores.append(store)
-    for copy, source, other, step in side:
-        copy.wait_recv()
-        there = lax.rem(lane - other + share, share)
-        store = pltpu.make_async_copy(held.at[source, there], out_ref.at[source, there], out_sem.at[step, other])
-        store.start()
-        stores.append(store)
-        sent.append(copy)
-    for copy in sent:
-        copy.wait_send()
-    for store in stores:
-        store.wait()
+        for way in ways:
+            if step < cols - 1:
+                @pl.when(passes_on(step, way))
+                def _(way=way):
+                    for piece in range(KVHEADS):
+                        on_copy(step, way, piece).wait_send()
+
+            if step or way == 1:
+                @pl.when(held_here(step, way))
+                def _(way=way):
+                    for other in range(share):
+                        if other:
+                            for piece in range(KVHEADS):
+                                side_copy(step, way, piece, other, False).wait_send()
+                        out_copy(step, way, other).wait()
 
 
 def spread(key, value, rows, cols):
@@ -126,11 +194,11 @@
             dma((2,)),
             dma((KVHEADS - 1, 2)),
             dma((KVHEADS - 1, 2)),
-            dma((cols - 1,)),
-            dma((cols - 1,)),
-            dma((cols, share - 1)),
-            dma((cols, share - 1)),
-            dma((cols, share)),
+            dma((cols - 1, 2, KVHEADS)),
+            dma((cols - 1, 2, KVHEADS)),
+            dma((cols, 2, KVHEADS, share - 1)),
+            dma((cols, 2, KVHEADS, share - 1)),
+            dma((cols, 2, share)),
         ],
         compiler_params=pltpu.CompilerParams(
             collective_id=0, has_side_effects=True, vmem_limit_bytes=VMEM_LIMIT
@@ -140,7 +208,7 @@
 
 
 def attend_kernel(cols, share, chunk_spans, order_ref, place_ref, query_ref, held_ref, out_ref,
-                  keys, values, queries, best, total):
+                  keys, values, queries, best, total, ahead):
     tokens = query_ref.shape[1]
     heads = query_ref.shape[2] // HEAD_DIM
     count = heads * tokens
@@ -156,8 +224,9 @@
             row, col = span // cols, span % cols
             spot = pl.ds(pl.multiple_of(order_ref[span] * tokens, tokens), tokens)
             block = held_ref[col, row % share, row // share, 0]
-            keys[spot, :HEAD_DIM] = block
-            keys[spot, HEAD_DIM:] = block
+            turned = block.astype(jnp.float32).T.astype(block.dtype)
+            keys[:HEAD_DIM, spot] = turned
+            keys[HEAD_DIM:, spot] = turned
             values[spot, :HEAD_DIM] = held_ref[col, row % share, row // share, 1]
             return carry
 
@@ -173,35 +242,38 @@
 
     mine = order_ref[step * cols + place_ref[1]]
     last = mine // chunk_spans
-    strip = 2 * tokens if heads % 2 == 0 else tokens
-
-    def chunk(index, first):
-        spot = pl.ds(pl.multiple_of(index * width, width), width)
-        for start in range(0, count, strip):
-            lines = slice(start, start + strip)
-            scores = lax.dot_general(
-                queries[lines, :], keys[spot, :], (((1,), (1,)), ((), ())), preferred_element_type=jnp.float32
-            )
-            if first:
-                below = lax.broadcasted_iota(jnp.int32, scores.shape, 0) % tokens
-                across = lax.broadcasted_iota(jnp.int32, scores.shape, 1)
-                scores = jnp.where(across <= below + (mine % chunk_spans) * tokens, scores, masked_score)
-                newest = jnp.max(scores, axis=1, keepdims=True)
-            else:
-                before = best[lines, :1]
-                newest = jnp.maximum(before, jnp.max(scores, axis=1, keepdims=True))
-            raised = jnp.exp2(scores - newest).astype(jnp.bfloat16)
-            update = jnp.dot(raised, values[spot, :], preferred_element_type=jnp.float32)
-            if first:
-                total[lines, :] = update
-            else:
-                total[lines, :] = total[lines, :] * jnp.exp2(before - newest) + update
-            best[lines, :] = jnp.broadcast_to(newest, (strip, HEAD_DIM))
-
-    chunk(last, True)
+
+    def spot(index):
+        return pl.ds(pl.multiple_of(index * width, width), width)
+
+    def score(index):
+        return jnp.dot(queries[...], keys[:, spot(index)], preferred_element_type=jnp.float32)
+
+    def top_of(scores):
+        return jnp.broadcast_to(jnp.max(scores, axis=1, keepdims=True), (count, HEAD_DIM))
+
+    def weigh(scores, newest, index):
+        raised = jnp.exp2(scores - jnp.concatenate([newest] * chunk_spans, axis=1)).astype(jnp.bfloat16)
+        return jnp.dot(raised, values[spot(index), :], preferred_element_type=jnp.float32)
+
+    scores = score(last)
+    below = lax.broadcasted_iota(jnp.int32, scores.shape, 0) % tokens
+    across = lax.broadcasted_iota(jnp.int32, scores.shape, 1)
+    scores = jnp.where(across <= below + (mine % chunk_spans) * tokens, scores, masked_score)
+    newest = top_of(scores)
+    ahead[...] = score(0)
+    total[...] = weigh(scores, newest, last)
+    best[...] = newest
 
     def body(index, carry):
-        chunk(index, False)
+        scores = ahead[...]
+        before = best[...]
+        newest = jnp.maximum(before, top_of(scores))
+        shrink = jnp.exp2(before - newest)
+        ahead[...] = score(jnp.minimum(index + 1, last))
+        update = weigh(scores, newest, index)
+        total[...] = total[...] * jnp.concatenate([shrink] * 2, axis=1) + update
+        best[...] = newest
         return carry
 
     lax.fori_loop(0, last, body, 0)
@@ -233,11 +305,12 @@
             ],
             out_specs=pl.BlockSpec((1, tokens, width), lambda step, order, place: (step, 0, 0)),
             scratch_shapes=[
-                pltpu.VMEM((sequence, 2 * HEAD_DIM), jnp.bfloat16),
+                pltpu.VMEM((2 * HEAD_DIM, sequence), jnp.bfloat16),
                 pltpu.VMEM((sequence, 2 * HEAD_DIM), jnp.bfloat16),
                 pltpu.VMEM((count, 2 * HEAD_DIM), jnp.bfloat16),
                 pltpu.VMEM((count, HEAD_DIM), jnp.float32),
                 pltpu.VMEM((count, 2 * HEAD_DIM), jnp.float32),
+                pltpu.VMEM((count, chunk_spans * tokens), jnp.float32),
             ],
         ),
         compiler_params=pltpu.CompilerParams(

time: 93.8 us -> 75.3 us (0.80)
  the two profiles are of different devices: /device:TPU:9 before, /device:TPU:1 now
where the time goes in v2:
time: 75.3 us; the launch traced here: 74 us
  Pallas kernels  71.1 us (94%)
  local copies, waits for them, and re-layouts  2.29 us (3%)
    pallas_call x1, Pallas kernels, spread(): pl.pallas_call(functools.partial(spread_kernel, rows, cols), out_shape=ja...  28 us
    pallas_call x1, Pallas kernels, attend(): pl.pallas_call(functools.partial(attend_kernel, cols, share, chunk_spans)...  26.8 us
    pallas_call x1, Pallas kernels, deliver(): pl.pallas_call(functools.partial(deliver_kernel, rows), out_shape=jax.Sha...  16.3 us
    unnamed x1, local copies, waits for them, and re-layouts  2.29 us

profile of v2, /device:TPU:1, one launch (start us, length us, event | category | flops | bytes accessed | tf_op | source)
XLA Modules:
  0.0 74.0 jit_solution(6393213282223474467)
XLA Ops:
  0.0 0.6 pad_add_fusion.place_ref
  0.6 28.0 %spread.1.held_ref = bf16[4,2,4,2,128,128]{5,4,3,2,1,0:T(8,128)(2,1)} custom-call(bf16[128,512]{1,0:T(8,128)(2,1)} %key_ref.1, bf16[128,512]{1,0:T(8,128)(2,1)} %value_ref.1), custom_call_target="tpu_custom_call" | custom-call | tf_op jit(solution)/shard_map/spread/pallas_call | solution.py:187
  28.6 26.8 %attend.1.part_ref = bf16[8,128,512]{2,1,0:T(8,128)(2,1)} custom-call(s32[32]{0:T(128)} %order_ref.1, s32[2]{0:T(128)} %pad_add_fusion.place_ref, bf16[8,128,4096]{2,1,0:T(8,128)(2,1)} %query_ref.1, bf16[4,2,4,2,128,128]{5,4,3,2,1,0:T(8,128)(2,1)} %spread.1.held_ref), custom_call_target="tpu_custom_call" | custom-call | tf_op jit(solution)/shard_map/attend/pallas_call | solution.py:296
  55.4 16.3 %deliver.1 = bf16[128,4096]{1,0:T(8,128)(2,1)} custom-call(bf16[8,128,512]{2,1,0:T(8,128)(2,1)} %attend.1.part_ref), custom_call_target="tpu_custom_call" | custom-call | tf_op jit(solution)/shard_map/deliver/pallas_call | solution.py:356
  71.7 2.3 %copy.6 = bf16[128,4096]{1,0:T(8,128)(2,1)} copy(bf16[128,4096]{1,0:T(8,128)(2,1)} %deliver.1) | data formatting | bytes 2097152

commit v3 on v2

--- a/solution.py
+++ b/solution.py
@@ -207,7 +207,7 @@
     )(key, value)
 
 
-def attend_kernel(cols, share, chunk_spans, order_ref, place_ref, query_ref, held_ref, out_ref,
+def attend_kernel(cols, share, chunk_spans, order_ref, query_ref, held_ref, out_ref,
                   keys, values, queries, best, total, ahead):
     tokens = query_ref.shape[1]
     heads = query_ref.shape[2] // HEAD_DIM
@@ -224,13 +224,13 @@
             row, col = span // cols, span % cols
             spot = pl.ds(pl.multiple_of(order_ref[span] * tokens, tokens), tokens)
             block = held_ref[col, row % share, row // share, 0]
-            turned = block.astype(jnp.float32).T.astype(block.dtype)
+            turned = block.T
             keys[:HEAD_DIM, spot] = turned
             keys[HEAD_DIM:, spot] = turned
             values[spot, :HEAD_DIM] = held_ref[col, row % share, row // share, 1]
             return carry
 
-        lax.fori_loop(0, spans, place, 0)
+        lax.fori_loop(0, spans, place, 0, unroll=8)
 
     scale = math.log2(math.e) / math.sqrt(HEAD_DIM)
     for head in range(heads):
@@ -240,7 +240,7 @@
         queries[head * tokens : (head + 1) * tokens, :HEAD_DIM] = high
         queries[head * tokens : (head + 1) * tokens, HEAD_DIM:] = low
 
-    mine = order_ref[step * cols + place_ref[1]]
+    mine = order_ref[step * cols + lax.axis_index("col")]
     last = mine // chunk_spans
 
     def spot(index):
@@ -292,18 +292,17 @@
     sequence = spans * tokens
     count = width // HEAD_DIM * tokens
     chunk_spans = 4
-    place = jnp.stack([lax.axis_index("row"), lax.axis_index("col")]).astype(jnp.int32)
     return pl.pallas_call(
         functools.partial(attend_kernel, cols, share, chunk_spans),
         out_shape=jax.ShapeDtypeStruct((rows, tokens, width), query.dtype),
         grid_spec=pltpu.PrefetchScalarGridSpec(
-            num_scalar_prefetch=2,
+            num_scalar_prefetch=1,
             grid=(rows,),
             in_specs=[
-                pl.BlockSpec((1, tokens, width), lambda step, order, place: (step, 0, place[0])),
-                pl.BlockSpec(held.shape, lambda step, order, place: (0,) * held.ndim),
+                pl.BlockSpec((1, tokens, width), lambda step, order: (step, 0, lax.axis_index("row"))),
+                pl.BlockSpec(held.shape, lambda step, order: (0,) * held.ndim),
             ],
-            out_specs=pl.BlockSpec((1, tokens, width), lambda step, order, place: (step, 0, 0)),
+            out_specs=pl.BlockSpec((1, tokens, width), lambda step, order: (step, 0, 0)),
             scratch_shapes=[
                 pltpu.VMEM((2 * HEAD_DIM, sequence), jnp.bfloat16),
                 pltpu.VMEM((sequence, 2 * HEAD_DIM), jnp.bfloat16),
@@ -317,7 +316,7 @@
             dimension_semantics=("arbitrary",), vmem_limit_bytes=VMEM_LIMIT
         ),
         name="attend",
-    )(span_order, place, query, held)
+    )(span_order, query, held)
 
 
 def deliver_kernel(rows, part_ref, out_ref, own_sem, send_sem, recv_sem):

time: 75.3 us -> 73.5 us (0.976); the launches traced: 74 us -> 75 us
  Pallas kernels: 71.1 us -> 72.7 us
    pallas_call x1, Pallas kernels: 26.8 us -> 28.4 us  [attend(): pl.pallas_call(functools.partial(attend_kernel, cols, share, chunk_spans)...]
where the time goes in v3:
time: 73.5 us; the launch traced here: 75 us
  Pallas kernels  72.7 us (99%)
  local copies, waits for them, and re-layouts  2.29 us (3%)
    pallas_call x1, Pallas kernels, attend(): pl.pallas_call(functools.partial(attend_kernel, cols, share, chunk_spans)...  28.4 us
    pallas_call x1, Pallas kernels, spread(): pl.pallas_call(functools.partial(spread_kernel, rows, cols), out_shape=ja...  28 us
    pallas_call x1, Pallas kernels, deliver(): pl.pallas_call(functools.partial(deliver_kernel, rows), out_shape=jax.Sha...  16.3 us
    unnamed x1, local copies, waits for them, and re-layouts  2.29 us

profile of v3, /device:TPU:1, one launch (start us, length us, event | category | flops | bytes accessed | tf_op | source)
XLA Modules:
  0.0 75.0 jit_solution(13517014239708502596)
XLA Ops:
  0.0 28.0 %spread.1.held_ref = bf16[4,2,4,2,128,128]{5,4,3,2,1,0:T(8,128)(2,1)} custom-call(bf16[128,512]{1,0:T(8,128)(2,1)} %key_ref.1, bf16[128,512]{1,0:T(8,128)(2,1)} %value_ref.1), custom_call_target="tpu_custom_call" | custom-call | tf_op jit(solution)/shard_map/spread/pallas_call | solution.py:187
  28.1 28.4 %attend.1.part_ref = bf16[8,128,512]{2,1,0:T(8,128)(2,1)} custom-call(s32[32]{0:T(128)} %order_ref.1, bf16[8,128,4096]{2,1,0:T(8,128)(2,1)} %query_ref.1, bf16[4,2,4,2,128,128]{5,4,3,2,1,0:T(8,128)(2,1)} %spread.1.held_ref), custom_call_target="tpu_custom_call" | custom-call | tf_op jit(solution)/shard_map/attend/pallas_call | solution.py:295
  56.4 16.3 %deliver.1 = bf16[128,4096]{1,0:T(8,128)(2,1)} custom-call(bf16[8,128,512]{2,1,0:T(8,128)(2,1)} %attend.1.part_ref), custom_call_target="tpu_custom_call" | custom-call | tf_op jit(solution)/shard_map/deliver/pallas_call | solution.py:355
  72.7 2.3 %copy.6 = bf16[128,4096]{1,0:T(8,128)(2,1)} copy(bf16[128,4096]{1,0:T(8,128)(2,1)} %deliver.1) | data formatting | bytes 2097152
